TPU v7x, 32 devices: a whole 2x2x4 slice. The times are simulated.
32 devices in a mesh: dp: 2 (over y), expert: 4 (over z), tensor: 4 (over x, core).
Axes of the slice: x: 2, y: 2, z: 4, core: 2. Of those that a mesh axis runs over, the one named last changes fastest.
Arguments:
- grad_out: bfloat16 [1024, 6144], P(('dp', 'expert'), 'tensor'), may hold values from -0.1875 to 0.1875
- expert_ids: int32 [1024, 2], P(('dp', 'expert')), may hold values from 0 to 3, all different within a row; in each aligned block of 128 rows (0 to 127, 128 to 255, ...) at most 64 rows name the same one
- route_gates: float32 [1024, 2], P(('dp', 'expert')), may hold values from 0.1 to 1
- saved_hidden: bfloat16 [4, 256, 16384], P('expert', 'dp', 'tensor'), may hold values from -6 to 6
Outputs:
- weight_grad: bfloat16 [4, 16384, 6144], P('expert', 'tensor', 'dp')
Inputs may be any that keep to these rules, and one draw needn't show every extreme that they name: `expert_ids`: each row names 2 different experts. Among the rows of one device no expert is named by more than 64 rows, and every expert is named somewhere.
All inputs are finite; a program needn't handle non-finite values.
Results may differ from a plain program's by a relative error of at most 0.0049.
Values may be sent and summed in bfloat16 or wider, within the bound.
A program may use at most 128 MiB of HBM per device.

v0:
```python
import jax
import jax.numpy as jnp
from jax import lax
from jax.sharding import PartitionSpec as P

TOP = 2
CAP = 32


def slot_table(expert_ids, route_gates, expert_count):
    routes = expert_ids.reshape(-1)
    weights = route_gates.reshape(-1)
    onehot = (routes[:, None] == jnp.arange(expert_count, dtype=jnp.int32)[None, :]).astype(
        jnp.int32
    )
    before = jnp.cumsum(onehot, axis=0) - onehot
    rank = jnp.sum(before * onehot, axis=1)
    target = jnp.where(rank < CAP, routes * CAP + rank, -1)
    match = jnp.arange(expert_count * CAP, dtype=jnp.int32)[:, None] == target[None, :]
    chosen = match.reshape(expert_count * CAP, -1, TOP).any(axis=2)
    slot_gate = jnp.sum(
        jnp.where(match, weights[None, :], jnp.zeros_like(weights)[None, :]), axis=1
    )
    return (chosen.astype(jnp.bfloat16), slot_gate)


def local(grad_out, expert_ids, route_gates, saved_hidden):
    data_count = lax.axis_size("dp")
    expert_count = lax.axis_size("expert")
    chosen, slot_gate = slot_table(expert_ids, route_gates, expert_count)
    width = grad_out.shape[1] * lax.axis_size("tensor")
    block_width = width // data_count
    complete = lax.all_gather(grad_out, "tensor", axis=1, tiled=True)
    parted = complete.reshape(complete.shape[0], data_count, block_width)
    picked = jnp.einsum("st,tdk->dsk", chosen, parted, preferred_element_type=jnp.float32)
    outgoing = (picked * slot_gate[None, :, None]).astype(jnp.bfloat16)
    outgoing = outgoing.reshape(data_count * expert_count, CAP, block_width)
    arrived = lax.all_to_all(outgoing, ("dp", "expert"), split_axis=0, concat_axis=0, tiled=True)
    received = arrived.reshape(-1, block_width)
    hidden = saved_hidden[0]
    summed = lax.dot_general(
        lax.all_gather(hidden, "dp", axis=0, tiled=True),
        received,
        (((0,), (0,)), ((), ())),
        preferred_element_type=jnp.float32,
    )
    return summed.astype(jnp.bfloat16)[None]


def solution(mesh):
    in_specs = (
        P(("dp", "expert"), "tensor"),
        P(("dp", "expert"), None),
        P(("dp", "expert"), None),
        P("expert", "dp", "tensor"),
    )
    out_specs = P("expert", "tensor", "dp")
    return jax.shard_map(local, mesh=mesh, in_specs=in_specs, out_specs=out_specs, check_vma=False)
```

profile of v0, /device:TPU:0, one launch (start us, length us, event | category | flops | bytes accessed | tf_op | source)
XLA Modules:
  0.0 138.0 jit_solution(6330740520513970459)
XLA Ops:
  7.4 0.0 all-gather.4.cloned.1.call-start
  7.4 1.9 %copy.26 = bf16[128,1536]{0,1:T(8,128)(2,1)} copy(bf16[128,1536]{1,0:T(8,128)(2,1)} %param.4) | data formatting | bytes 786432 | tf_op args[0]
  9.3 0.0 all-gather.4.cloned.1.call-update
  9.3 0.8 copy.19
  10.1 0.1 eq.46
  10.2 0.1 eq.50
  10.4 0.7 broadcast_multiply_fusion
  11.1 0.1 copy.24
  11.2 1.2 reduce-window.6
  12.4 0.1 slice.8
  12.5 0.1 copy.21
  12.6 0.1 copy.22
  12.7 0.1 add_bitcast_fusion
  12.8 0.1 reduce_sum.21
  13.0 0.1 copy.25
  13.1 0.8 copy.28
  13.9 0.1 broadcast_in_dim.33
  14.0 0.1 select_reduce_fusion
  14.2 18.0 %all-gather.4.cloned.1.call-done = bf16[128,6144]{0,1:T(8,128)(2,1)} async-done(((bf16[128,1536]{0,1:T(8,128)(2,1)}), bf16[128,6144]{0,1:T(8,128)(2,1)}) %all-gather.4.cloned.1.call-update) | async-done | bytes 1572880 | tf_op jit(solution)/shard_map/all_gather | solution.py:33
  32.1 3.1 %fusion = bf16[128,2,3072]{2,0,1:T(8,128)(2,1)} fusion(bf16[128,2,3072]{0,2,1:T(8,128)(2,1)} %bitcast.37, f32[128]{0:T(128)S(1)} %select_reduce_fusion, pred[128,128]{1,0:T(8,128)(4,1)S(1)} %fusion.2), kind=kOutput, calls=%fused_computation.2 | convolution fusion | flops 202899456 | bytes 3162624 | tf_op jit(solution)/shard_map/st,tdk->dsk/dot_general | solution.py:35
  35.2 5.5 %all-to-all-start = ((bf16[8,32,3072]{2,1,0:T(8,128)(2,1)}), bf16[8,32,3072]{2,1,0:T(8,128)(2,1)S(1)}, u32[]{:S(2)}, u32[]{:S(2)}) async-start(bf16[8,32,3072]{2,1,0:T(8,128)(2,1)} %bitcast.5), calls=%async_computation | async-start | bytes 3145728 | tf_op jit(solution)/shard_map/all_to_all | solution.py:38
  40.8 0.0 all-gather.6.cloned.1.call-start
  40.8 0.5 all-gather.6.cloned.1.call-update
  41.3 43.3 %all-gather.6.cloned.1.call-done = bf16[1,256,4096]{2,1,0:T(8,128)(2,1)} async-done(((bf16[1,128,4096]{2,1,0:T(8,128)(2,1)}), bf16[1,256,4096]{2,1,0:T(8,128)(2,1)}) %all-gather.6.cloned.1.call-update) | async-done | bytes 2097168 | tf_op jit(solution)/shard_map/all_gather | solution.py:42
  84.7 0.0 all-to-all-done
  84.7 13.3 %convert_bitcast_fusion = bf16[1,4096,3072]{1,2,0:T(8,128)(2,1)} fusion(bf16[256,3072]{1,0:T(8,128)(2,1)S(1)} %bitcast.36, bf16[1,256,4096]{2,1,0:T(8,128)(2,1)} %all-gather.6.cloned.1.call-done), kind=kOutput, calls=%fused_computation | convolution fusion | flops 6455033856 | bytes 28835840 | tf_op jit(solution)/shard_map/dot_general | solution.py:41
  98.0 32.6 %copy.29 = bf16[1,4096,3072]{2,1,0:T(8,128)(2,1)} copy(bf16[1,4096,3072]{1,2,0:T(8,128)(2,1)} %convert_bitcast_fusion) | data formatting | bytes 50331648 | tf_op jit(solution)/shard_map/broadcast_in_dim | solution.py:47
  (7 shorter events, 0.1 us)
Async XLA Ops:
  7.4 24.7 %all-gather.4.cloned.1.call-start = ((), (), s32[]{:S(2)}) async-start(), calls=%async_computation.1 | async-start | bytes 1966080 | tf_op jit(solution)/shard_map/all_gather | solution.py:33
  35.2 49.4 %all-to-all-start = ((bf16[8,32,3072]{2,1,0:T(8,128)(2,1)}), bf16[8,32,3072]{2,1,0:T(8,128)(2,1)S(1)}, u32[]{:S(2)}, u32[]{:S(2)}) async-start(bf16[8,32,3072]{2,1,0:T(8,128)(2,1)} %bitcast.5), calls=%async_computation | async-start | bytes 3145728 | tf_op jit(solution)/shard_map/all_to_all | solution.py:38
  40.8 43.9 %all-gather.6.cloned.1.call-start = ((), (), s32[]{:S(2)}) async-start(), calls=%async_computation.2 | async-start | bytes 3145728 | tf_op jit(solution)/shard_map/all_gather | solution.py:42
Sparse Core Ops, SparseCore 0:
  9.7 22.3 all-gather.3
Sparse Core Ops, SparseCore 1:
  42.8 41.8 all-gather.5
where the time goes:
time: 139 us; the launch traced here: 138 us
  waiting for transfers between devices  61.8 us (44%)
  local copies, waits for them, and re-layouts  37.1 us (27%)
  matrix products  16.4 us (12%)
  between operations  14.9 us (11%)
  starting transfers between devices  5.56 us (4%)
  other arithmetic  2.2 us (2%)
    all_gather x1, waiting for transfers between devices, local(): lax.all_gather(hidden, 'dp', axis=0, tiled=True)  43.3 us
    broadcast_in_dim x1, local copies, waits for them, and re-layouts, local(): return summed.astype(jnp.bfloat16)[None]  32.6 us
    all_gather x1, waiting for transfers between devices, local(): complete = lax.all_gather(grad_out, 'tensor', axis=1, tiled=True)  18 us
    dot_general x1, matrix products, local(): lax.dot_general(lax.all_gather(hidden, 'dp', axis=0, tiled=True), receive...  13.3 us
    all_to_all x1, starting transfers between devices, local(): lax.all_to_all(outgoing, ('dp', 'expert'), split_axis=0, concat_axis=0, t...  5.52 us
    unnamed x3, local copies, waits for them, and re-layouts  3.51 us
    dot_general x1, matrix products, local(): jnp.einsum('st,tdk->dsk', chosen, parted, preferred_element_type=jnp.floa...  3.13 us
  transfers between devices with their start and end apart: 3, of which 2 were waited for; matrix products, arithmetic and copies ran while one was open for 3% of the time, Pallas kernels for 0%

commit v1 on v0

--- a/solution.py
+++ b/solution.py
@@ -1,10 +1,16 @@
+import functools
+
 import jax
 import jax.numpy as jnp
 from jax import lax
+from jax.experimental import pallas as pl
+from jax.experimental.pallas import tpu as pltpu
 from jax.sharding import PartitionSpec as P
 
 TOP = 2
 CAP = 32
+MESH = pl.DeviceIdType.MESH
+TN = (((0,), (0,)), ((), ()))
 
 
 def slot_table(expert_ids, route_gates, expert_count):
@@ -24,7 +30,7 @@
     return (chosen.astype(jnp.bfloat16), slot_gate)
 
 
-def local(grad_out, expert_ids, route_gates, saved_hidden):
+def plain(grad_out, expert_ids, route_gates, saved_hidden):
     data_count = lax.axis_size("dp")
     expert_count = lax.axis_size("expert")
     chosen, slot_gate = slot_table(expert_ids, route_gates, expert_count)
@@ -37,14 +43,240 @@
     outgoing = outgoing.reshape(data_count * expert_count, CAP, block_width)
     arrived = lax.all_to_all(outgoing, ("dp", "expert"), split_axis=0, concat_axis=0, tiled=True)
     received = arrived.reshape(-1, block_width)
+    summed = lax.dot_general(
+        lax.all_gather(saved_hidden[0], "dp", axis=0, tiled=True),
+        received,
+        TN,
+        preferred_element_type=jnp.float32,
+    )
+    return summed.astype(jnp.bfloat16)[None]
+
+
+def slot_rows(ids, gates, grad, experts):
+    tokens = ids.shape[1]
+    named, gate, rank = [], [], []
+    for e in range(experts):
+        first = (ids[0:1, :] == e).astype(jnp.float32)
+        second = (ids[1:2, :] == e).astype(jnp.float32)
+        named.append(jnp.broadcast_to(first + second, (CAP, tokens)))
+        gate.append(jnp.broadcast_to(first * gates[0:1, :] + second * gates[1:2, :], (CAP, tokens)))
+        rank.append(lax.broadcasted_iota(jnp.int32, (CAP, tokens), 0))
+    named = jnp.concatenate(named, axis=0)
+    gate = jnp.concatenate(gate, axis=0)
+    rank = jnp.concatenate(rank, axis=0).astype(jnp.float32)
+    row = lax.broadcasted_iota(jnp.int32, (tokens, tokens), 0)
+    column = lax.broadcasted_iota(jnp.int32, (tokens, tokens), 1)
+    earlier = jnp.where(row < column, 1.0, 0.0).astype(jnp.bfloat16)
+    before = jnp.dot(named.astype(jnp.bfloat16), earlier, preferred_element_type=jnp.float32)
+    chosen = jnp.where(before == rank, named, 0.0)
+    slot_gate = jnp.sum(chosen * gate, axis=1, keepdims=True)
+    picked = jnp.dot(chosen.astype(jnp.bfloat16), grad, preferred_element_type=jnp.float32)
+    return (picked * slot_gate).astype(jnp.bfloat16)
+
+
+def exchange(
+    D, E, T, cuts, ids_ref, gates_ref, grad_ref, hidden_ref, g_ref, other_ref, slots,
+    h_send, h_recv, s1, r1, s2, r2, s3, r3,
+):
+    d, e, t = lax.axis_index("dp"), lax.axis_index("expert"), lax.axis_index("tensor")
+    q = T // D
+    x, c = t // q, t % q
+    cols = grad_ref.shape[1]
+    W = cols // D
+    rows = hidden_ref.shape[0]
+
+    def hidden_copy(n, i):
+        lo, hi = cuts[i], cuts[i + 1]
+        return pltpu.make_async_remote_copy(
+            src_ref=hidden_ref.at[pl.ds(lo, hi - lo), :],
+            dst_ref=other_ref.at[pl.ds((D - n - 1) * rows + lo, hi - lo), :],
+            send_sem=h_send.at[n - 1, i],
+            recv_sem=h_recv.at[D - n - 1, i],
+            device_id=((d + n) % D, e, t),
+            device_id_type=MESH,
+        )
+
+    for n in range(1, D):
+        hidden_copy(n, 0).start()
+
+    slots[...] = slot_rows(ids_ref[...], gates_ref[...], grad_ref[...], E)
+
+    def place(r, source, x_at, c_at):
+        return g_ref.at[
+            pl.ds(pl.multiple_of(r * (E * CAP) + source * CAP, CAP), CAP),
+            pl.ds(pl.multiple_of(c_at * cols + x_at * W, 128), W),
+        ]
+
+    def first(j, m):
+        e2, x2 = (e + j) % E, (x + m) % D
+        r = (d - x + D) % D
+        src = slots.at[
+            pl.ds(pl.multiple_of(e2 * CAP, CAP), CAP), pl.ds(pl.multiple_of(x2 * W, 128), W)
+        ]
+        return src, place(r, e, x2, c), r1.at[r, (E - j) % E], (x, e2, x2 * q + c)
+
+    def first_remote(j, m):
+        src, dst, sem, to = first(j, m)
+        return pltpu.make_async_remote_copy(
+            src_ref=src, dst_ref=dst, send_sem=s1.at[j, m], recv_sem=sem,
+            device_id=to, device_id_type=MESH,
+        )
+
+    def first_local():
+        src = slots.at[
+            pl.ds(pl.multiple_of(e * CAP, CAP), CAP), pl.ds(pl.multiple_of(x * W, 128), W)
+        ]
+        return pltpu.make_async_copy(src, place(0, e, x, c), r1.at[0, 0])
+
+    order = sorted(range(E), key=lambda j: -min(j, E - j))
+    for j in order:
+        for m in range(D):
+            if j == 0 and m == 0:
+                pl.when(x == d)(lambda: first_local().start())
+                pl.when(x != d)(lambda: first_remote(0, 0).start())
+            else:
+                first_remote(j, m).start()
+
+    for i in range(1, len(cuts) - 1):
+        for n in range(1, D):
+            hidden_copy(n, i).start()
+
+    def along(n, r, k):
+        here = place(r, (e + k) % E, x, c)
+        return pltpu.make_async_remote_copy(
+            src_ref=here, dst_ref=here, send_sem=s2.at[n - 1, r, k], recv_sem=r2.at[D - n - 1, r, k],
+            device_id=(d, e, ((x + n) % D) * q + c), device_id_type=MESH,
+        )
+
+    def along_arrived(n, r, k):
+        here = place(r, (e + k) % E, (x + n) % D, c)
+        return pltpu.make_async_remote_copy(
+            src_ref=here, dst_ref=here, send_sem=s2.at[n - 1, r, k], recv_sem=r2.at[n - 1, r, k],
+            device_id=(d, e, ((x + n) % D) * q + c), device_id_type=MESH,
+        )
+
+    def across(p, n, r, k):
+        here = place(r, (e + k) % E, (x + n) % D, c)
+        return pltpu.make_async_remote_copy(
+            src_ref=here, dst_ref=here, send_sem=s3.at[p - 1, n, r, k],
+            recv_sem=r3.at[q - p - 1, n, r, k],
+            device_id=(d, e, x * q + (c + p) % q), device_id_type=MESH,
+        )
+
+    def across_arrived(p, n, r, k):
+        here = place(r, (e + k) % E, (x + n) % D, (c + p) % q)
+        return pltpu.make_async_remote_copy(
+            src_ref=here, dst_ref=here, send_sem=s3.at[p - 1, n, r, k],
+            recv_sem=r3.at[p - 1, n, r, k],
+            device_id=(d, e, x * q + (c + p) % q), device_id_type=MESH,
+        )
+
+    def first_arrived(r, k):
+        here = place(r, (e + k) % E, x, c)
+        return pltpu.make_async_remote_copy(
+            src_ref=here, dst_ref=here, send_sem=s1.at[0, 0], recv_sem=r1.at[r, k],
+            device_id=((d + r) % D, (e + k) % E, d * q + c), device_id_type=MESH,
+        )
+
+    blocks = [(r, k) for k in reversed(order) for r in range(D)]
+    for r, k in blocks:
+        if r == 0 and k == 0:
+            pl.when(x == d)(lambda: first_local().wait())
+            pl.when(x != d)(lambda: first_arrived(0, 0).wait_recv())
+        else:
+            first_arrived(r, k).wait_recv()
+        for n in range(1, D):
+            along(n, r, k).start()
+        for p in range(1, q):
+            across(p, 0, r, k).start()
+    for r, k in blocks:
+        for n in range(1, D):
+            along_arrived(n, r, k).wait_recv()
+            for p in range(1, q):
+                across(p, n, r, k).start()
+    for r, k in blocks:
+        for p in range(1, q):
+            for n in range(D):
+                across_arrived(p, n, r, k).wait_recv()
+    for j in order:
+        for m in range(D):
+            if j == 0 and m == 0:
+                pl.when(x != d)(lambda: first_remote(0, 0).wait_send())
+            else:
+                first_remote(j, m).wait_send()
+    for r, k in blocks:
+        for n in range(1, D):
+            along(n, r, k).wait_send()
+        for p in range(1, q):
+            for n in range(D):
+                across(p, n, r, k).wait_send()
+    for i in range(len(cuts) - 1):
+        for n in range(1, D):
+            hidden_copy(n, i).wait_send()
+            pltpu.make_async_remote_copy(
+                src_ref=hidden_ref.at[pl.ds(cuts[i], cuts[i + 1] - cuts[i]), :],
+                dst_ref=other_ref.at[pl.ds((n - 1) * rows + cuts[i], cuts[i + 1] - cuts[i]), :],
+                send_sem=h_send.at[n - 1, i],
+                recv_sem=h_recv.at[n - 1, i],
+                device_id=((d + n) % D, e, t),
+                device_id_type=MESH,
+            ).wait_recv()
+
+
+def product(strip, own_ref, other_ref, g_ref, o_ref):
+    hidden = jnp.concatenate([own_ref[...], other_ref[...]], axis=0)
+    for lo in range(0, g_ref.shape[1], strip):
+        o_ref[:, lo:lo + strip] = lax.dot_general(
+            hidden, g_ref[:, lo:lo + strip], TN, preferred_element_type=jnp.float32
+        ).astype(o_ref.dtype)
+
+
+def local(grad_out, expert_ids, route_gates, saved_hidden):
+    D, E, T = lax.axis_size("dp"), lax.axis_size("expert"), lax.axis_size("tensor")
+    tokens, cols = grad_out.shape
+    rows, units = saved_hidden.shape[1:]
+    depth = D * E * CAP
+    width = cols * T // D
+    tile, strip = 512, 1024
+    if T % D or cols % (128 * D) or units % tile or width % strip or rows != E * CAP or tokens % 128:
+        return plain(grad_out, expert_ids, route_gates, saved_hidden)
+    q = T // D
     hidden = saved_hidden[0]
-    summed = lax.dot_general(
-        lax.all_gather(hidden, "dp", axis=0, tiled=True),
-        received,
-        (((0,), (0,)), ((), ())),
-        preferred_element_type=jnp.float32,
-    )
-    return summed.astype(jnp.bfloat16)[None]
+    cuts = (0, rows // 4, rows)
+    pieces = len(cuts) - 1
+    vmem = pl.BlockSpec(memory_space=pltpu.VMEM)
+    hbm = pl.BlockSpec(memory_space=pl.ANY)
+    dma = pltpu.SemaphoreType.DMA
+    g, other = pl.pallas_call(
+        functools.partial(exchange, D, E, T, cuts),
+        out_shape=(
+            jax.ShapeDtypeStruct((depth, width), jnp.bfloat16),
+            jax.ShapeDtypeStruct(((D - 1) * rows, units), jnp.bfloat16),
+        ),
+        in_specs=[vmem, vmem, vmem, hbm],
+        out_specs=(vmem, hbm),
+        scratch_shapes=[
+            pltpu.VMEM((E * CAP, cols), jnp.bfloat16),
+            dma((D - 1, pieces)), dma((D - 1, pieces)),
+            dma((E, D)), dma((D, E)),
+            dma((D - 1, D, E)), dma((D - 1, D, E)),
+            dma((q - 1, D, D, E)), dma((q - 1, D, D, E)),
+        ],
+        compiler_params=pltpu.CompilerParams(has_side_effects=True),
+    )(expert_ids.T, route_gates.T, grad_out, hidden)
+    summed = pl.pallas_call(
+        functools.partial(product, strip),
+        grid=(units // tile,),
+        out_shape=jax.ShapeDtypeStruct((units, width), jnp.bfloat16),
+        in_specs=[
+            pl.BlockSpec((rows, tile), lambda i: (0, i)),
+            pl.BlockSpec(((D - 1) * rows, tile), lambda i: (0, i)),
+            pl.BlockSpec((depth, width), lambda i: (0, 0)),
+        ],
+        out_specs=pl.BlockSpec((tile, width), lambda i: (i, 0)),
+        compiler_params=pltpu.CompilerParams(dimension_semantics=("arbitrary",)),
+    )(hidden, other, g)
+    return summed[None]
 
 
 def solution(mesh):

time: 139 us -> 53.6 us (0.39)
  waiting for transfers between devices: 61.8 us -> 0 us
  Pallas kernels: 0 us -> 53.3 us
  local copies, waits for them, and re-layouts: 37.1 us -> 0 us
  matrix products: 16.4 us -> 0 us
  between operations: 14.9 us -> 0.01 us
  starting transfers between devices: 5.56 us -> 0 us
  other arithmetic: 2.2 us -> 0 us
    all_gather x2 -> x0, waiting for transfers between devices: 61.3 us -> none  [the longest x1 43.3 us: local(): lax.all_gather(hidden, 'dp', axis=0, tiled=True)]
    pallas_call x0 -> x2, Pallas kernels: none -> 53.3 us  [the longest x1 39.8 us: local(): pl.pallas_call(functools.partial(exchange, D, E, T, cuts), out_shape=(jax...]
    broadcast_in_dim x2 -> x0, local copies, waits for them, and re-layouts: 32.7 us -> none  [the longest x1 32.6 us: local(): return summed.astype(jnp.bfloat16)[None]]
    dot_general x2 -> x0, matrix products: 16.4 us -> none  [the longest x1 13.3 us: local(): lax.dot_general(lax.all_gather(hidden, 'dp', axis=0, tiled=True), receive...]
    all_to_all x1 -> x0, starting transfers between devices: 5.52 us -> none  [local(): lax.all_to_all(outgoing, ('dp', 'expert'), split_axis=0, concat_axis=0, t...]
    unnamed x3 -> x0, local copies, waits for them, and re-layouts: 3.51 us -> none
  transfers between devices with their start and end apart: 3 -> 0, of which waited for: 2 -> 0; matrix products, arithmetic and copies ran while one was open for 3% -> 0% of each run, Pallas kernels for 0% -> 0%
where the time goes in v1:
time: 53.6 us; the launch traced here: 53.3 us
  Pallas kernels  53.3 us (99%)
    pallas_call x1, Pallas kernels, local(): pl.pallas_call(functools.partial(exchange, D, E, T, cuts), out_shape=(jax...  39.8 us
    pallas_call x1, Pallas kernels, local(): pl.pallas_call(functools.partial(product, strip), grid=(units // tile,),...  13.6 us

profile of v1, /device:TPU:0, one launch (start us, length us, event | category | flops | bytes accessed | tf_op | source)
XLA Modules:
  0.0 53.3 jit_solution(10142794481838086576)
XLA Ops:
  0.0 39.8 %shard_map.46 = (bf16[256,3072]{1,0:T(8,128)(2,1)}, bf16[128,4096]{1,0:T(8,128)(2,1)}) custom-call(s32[2,128]{1,0:T(2,128)} %bitcast.6, f32[2,128]{1,0:T(2,128)} %bitcast.7, bf16[128,1536]{1,0:T(8,128)(2,1)} %grad_ref.1, bf16[128,4096]{1,0:T(8,128)(2,1)} %bitcast.4), custom_call_target="tpu_custom_call" | custom-call | tf_op jit(solution)/shard_map/pallas_call | solution.py:250
  39.8 13.6 %shard_map.47 = bf16[4096,3072]{1,0:T(8,128)(2,1)} custom-call(bf16[128,4096]{1,0:T(8,128)(2,1)} %bitcast.5, bf16[128,4096]{1,0:T(8,128)(2,1)} %get-tuple-element.7.other_ref, bf16[256,3072]{1,0:T(8,128)(2,1)} %get-tuple-element.8.g_ref), custom_call_target="tpu_custom_call" | custom-call | tf_op jit(solution)/shard_map/pallas_call | solution.py:267

commit v2 on v1

--- a/solution.py
+++ b/solution.py
@@ -237,7 +237,7 @@
     rows, units = saved_hidden.shape[1:]
     depth = D * E * CAP
     width = cols * T // D
-    tile, strip = 512, 1024
+    tile, strip = 1024, 1024
     if T % D or cols % (128 * D) or units % tile or width % strip or rows != E * CAP or tokens % 128:
         return plain(grad_out, expert_ids, route_gates, saved_hidden)
     q = T // D

time: 53.6 us -> 52.7 us (0.983)
  Pallas kernels: 53.3 us -> 52.5 us
    pallas_call x1, Pallas kernels: 13.6 us -> 12.8 us  [local(): pl.pallas_call(functools.partial(product, strip), grid=(units // tile,),...]
where the time goes in v2:
time: 52.7 us; the launch traced here: 52.5 us
  Pallas kernels  52.5 us (100%)
    pallas_call x1, Pallas kernels, local(): pl.pallas_call(functools.partial(exchange, D, E, T, cuts), out_shape=(jax...  39.8 us
    pallas_call x1, Pallas kernels, local(): pl.pallas_call(functools.partial(product, strip), grid=(units // tile,),...  12.8 us

profile of v2, /device:TPU:0, one launch (start us, length us, event | category | flops | bytes accessed | tf_op | source)
XLA Modules:
  0.0 52.5 jit_solution(13670852479103348910)
XLA Ops:
  0.0 39.8 %shard_map.46 = (bf16[256,3072]{1,0:T(8,128)(2,1)}, bf16[128,4096]{1,0:T(8,128)(2,1)}) custom-call(s32[2,128]{1,0:T(2,128)} %bitcast.6, f32[2,128]{1,0:T(2,128)} %bitcast.7, bf16[128,1536]{1,0:T(8,128)(2,1)} %grad_ref.1, bf16[128,4096]{1,0:T(8,128)(2,1)} %bitcast.4), custom_call_target="tpu_custom_call" | custom-call | tf_op jit(solution)/shard_map/pallas_call | solution.py:250
  39.8 12.8 %shard_map.47 = bf16[4096,3072]{1,0:T(8,128)(2,1)} custom-call(bf16[128,4096]{1,0:T(8,128)(2,1)} %bitcast.5, bf16[128,4096]{1,0:T(8,128)(2,1)} %get-tuple-element.7.other_ref, bf16[256,3072]{1,0:T(8,128)(2,1)} %get-tuple-element.8.g_ref), custom_call_target="tpu_custom_call" | custom-call | tf_op jit(solution)/shard_map/pallas_call | solution.py:267

commit v3 on v2

--- a/solution.py
+++ b/solution.py
@@ -83,12 +83,12 @@
     x, c = t // q, t % q
     cols = grad_ref.shape[1]
     W = cols // D
-    rows = hidden_ref.shape[0]
+    rows, kept = hidden_ref.shape[0], other_ref.shape[1]
 
     def hidden_copy(n, i):
         lo, hi = cuts[i], cuts[i + 1]
         return pltpu.make_async_remote_copy(
-            src_ref=hidden_ref.at[pl.ds(lo, hi - lo), :],
+            src_ref=hidden_ref.at[pl.ds(lo, hi - lo), pl.ds(0, kept)],
             dst_ref=other_ref.at[pl.ds((D - n - 1) * rows + lo, hi - lo), :],
             send_sem=h_send.at[n - 1, i],
             recv_sem=h_recv.at[D - n - 1, i],
@@ -214,7 +214,7 @@
         for n in range(1, D):
             hidden_copy(n, i).wait_send()
             pltpu.make_async_remote_copy(
-                src_ref=hidden_ref.at[pl.ds(cuts[i], cuts[i + 1] - cuts[i]), :],
+                src_ref=hidden_ref.at[pl.ds(cuts[i], cuts[i + 1] - cuts[i]), pl.ds(0, kept)],
                 dst_ref=other_ref.at[pl.ds((n - 1) * rows + cuts[i], cuts[i + 1] - cuts[i]), :],
                 send_sem=h_send.at[n - 1, i],
                 recv_sem=h_recv.at[n - 1, i],
@@ -238,7 +238,7 @@
     depth = D * E * CAP
     width = cols * T // D
     tile, strip = 1024, 1024
-    if T % D or cols % (128 * D) or units % tile or width % strip or rows != E * CAP or tokens % 128:
+    if T % D or cols % (128 * D) or units % tile or units == tile or width % strip or rows != E * CAP or tokens % 128:
         return plain(grad_out, expert_ids, route_gates, saved_hidden)
     q = T // D
     hidden = saved_hidden[0]
@@ -251,7 +251,7 @@
         functools.partial(exchange, D, E, T, cuts),
         out_shape=(
             jax.ShapeDtypeStruct((depth, width), jnp.bfloat16),
-            jax.ShapeDtypeStruct(((D - 1) * rows, units), jnp.bfloat16),
+            jax.ShapeDtypeStruct(((D - 1) * rows, units - tile), jnp.bfloat16),
         ),
         in_specs=[vmem, vmem, vmem, hbm],
         out_specs=(vmem, hbm),
@@ -264,18 +264,35 @@
         ],
         compiler_params=pltpu.CompilerParams(has_side_effects=True),
     )(expert_ids.T, route_gates.T, grad_out, hidden)
-    summed = pl.pallas_call(
-        functools.partial(product, strip),
-        grid=(units // tile,),
-        out_shape=jax.ShapeDtypeStruct((units, width), jnp.bfloat16),
-        in_specs=[
-            pl.BlockSpec((rows, tile), lambda i: (0, i)),
-            pl.BlockSpec(((D - 1) * rows, tile), lambda i: (0, i)),
-            pl.BlockSpec((depth, width), lambda i: (0, 0)),
-        ],
-        out_specs=pl.BlockSpec((tile, width), lambda i: (i, 0)),
-        compiler_params=pltpu.CompilerParams(dimension_semantics=("arbitrary",)),
-    )(hidden, other, g)
+    tail, g, other = lax.optimization_barrier((hidden[:, units - tile:], g, other))
+    moved = jnp.concatenate(
+        [lax.ppermute(tail, "dp", [(s, (s - n) % D) for s in range(D)]) for n in range(1, D)]
+    )
+
+    def multiply(first, count, other_part, *into):
+        return pl.pallas_call(
+            lambda own_ref, other_ref, g_ref, *rest: product(
+                strip, own_ref, other_ref, g_ref, rest[-1]
+            ),
+            grid=(count,),
+            out_shape=jax.ShapeDtypeStruct((units, width), jnp.bfloat16),
+            in_specs=[
+                pl.BlockSpec((rows, tile), lambda i: (0, first + i)),
+                pl.BlockSpec(((D - 1) * rows, tile), lambda i: (0, i)),
+                pl.BlockSpec((depth, width), lambda i: (0, 0)),
+            ] + [hbm] * len(into),
+            out_specs=pl.BlockSpec((tile, width), lambda i: (first + i, 0)),
+            input_output_aliases={3: 0} if into else {},
+            compiler_params=pltpu.CompilerParams(dimension_semantics=("arbitrary",)),
+            cost_estimate=pl.CostEstimate(
+                flops=2 * count * tile * width * depth,
+                bytes_accessed=2 * count * tile * width,
+                transcendentals=0,
+            ),
+        )(hidden, other_part, g, *into)
+
+    begun = multiply(0, units // tile - 1, other)
+    summed = multiply(units // tile - 1, 1, moved, begun)
     return summed[None]
 
 

time: 52.7 us -> 53.3 us (1.011)
  local copies, waits for them, and re-layouts: 0 us -> 1.66 us
  Pallas kernels: 52.5 us -> 51 us
    pallas_call x1, Pallas kernels: 39.8 us -> 34.2 us  [local(): pl.pallas_call(functools.partial(exchange, D, E, T, cuts), out_shape=(jax...]
    pallas_call x1 -> x2, Pallas kernels: 12.8 us -> 16.8 us  [multiply(): pl.pallas_call(lambda own_ref, other_ref, g_ref, *rest: product(strip, ow...]
    slice x0 -> x1, local copies, waits for them, and re-layouts: none -> 0.97 us  [local(): hidden[:, units - tile:]]
    unnamed x0 -> x2, local copies, waits for them, and re-layouts: none -> 0.7 us
  transfers between devices with their start and end apart: 0 -> 1, of which waited for: 0 -> 0; matrix products, arithmetic and copies ran while one was open for 0% -> 0% of each run, Pallas kernels for 0% -> 20%
where the time goes in v3:
time: 53.3 us; the launch traced here: 53.1 us
  Pallas kernels  51 us (96%)
  local copies, waits for them, and re-layouts  1.66 us (3%)
    pallas_call x1, Pallas kernels, local(): pl.pallas_call(functools.partial(exchange, D, E, T, cuts), out_shape=(jax...  34.2 us
    pallas_call x2, Pallas kernels, multiply(): pl.pallas_call(lambda own_ref, other_ref, g_ref, *rest: product(strip, ow...  16.8 us
  transfers between devices with their start and end apart: 1, of which 0 were waited for; matrix products, arithmetic and copies ran while one was open for 0% of the time, Pallas kernels for 20%

profile of v3, /device:TPU:0, one launch (start us, length us, event | category | flops | bytes accessed | tf_op | source)
XLA Modules:
  0.0 53.1 jit_solution(15693933629345728314)
XLA Ops:
  0.0 1.0 %slice.4 = bf16[128,1024]{1,0:T(8,128)(2,1)S(1)} slice(bf16[128,4096]{1,0:T(8,128)(2,1)} %bitcast.4), slice={[0:128], [3072:4096]} | slice | bytes 524288 | tf_op jit(solution)/shard_map/slice | solution.py:267
  1.0 34.2 %shard_map.46 = (bf16[256,3072]{1,0:T(8,128)(2,1)}, bf16[128,3072]{1,0:T(8,128)(2,1)}) custom-call(s32[2,128]{1,0:T(2,128)} %bitcast.8, f32[2,128]{1,0:T(2,128)} %bitcast.9, bf16[128,1536]{1,0:T(8,128)(2,1)} %grad_ref.1, bf16[128,4096]{1,0:T(8,128)(2,1)} %bitcast.5), custom_call_target="tpu_custom_call" | custom-call | tf_op jit(solution)/shard_map/pallas_call | solution.py:250
  35.2 0.5 collective-permute-start
  35.6 10.7 %shard_map.47.rest_0_ = bf16[4096,3072]{1,0:T(8,128)(2,1)} custom-call(bf16[128,4096]{1,0:T(8,128)(2,1)} %bitcast.6, bf16[128,3072]{1,0:T(8,128)(2,1)} %get-tuple-element.14.other_ref, bf16[256,3072]{1,0:T(8,128)(2,1)} %get-tuple-element.13.g_ref), custom_call_target="tpu_custom_call" | custom-call | flops 4831838208 | bytes 18874368 | tf_op jit(solution)/shard_map/pallas_call | solution.py:273
  46.3 0.0 collective-permute-done.other_ref
  46.3 0.0 copy-start
  46.3 0.7 %copy-done = bf16[128,1024]{1,0:T(8,128)(2,1)} copy-done((bf16[128,1024]{1,0:T(8,128)(2,1)}, bf16[128,1024]{1,0:T(8,128)(2,1)S(1)}, u32[]{:S(2)}) %copy-start) | copy-done | bytes 262168
  47.0 6.1 %shard_map.48 = bf16[4096,3072]{1,0:T(8,128)(2,1)} custom-call(bf16[128,4096]{1,0:T(8,128)(2,1)} %bitcast.7, bf16[128,1024]{1,0:T(8,128)(2,1)} %copy-done, bf16[256,3072]{1,0:T(8,128)(2,1)} %get-tuple-element.13.g_ref, bf16[4096,3072]{1,0:T(8,128)(2,1)} %shard_map.47.rest_0_), custom_call_target="tpu_custom_call", output_to_operand_aliasing={{}: (3, {})} | custom-call | flops 1610612736 | bytes 6291456 | tf_op jit(solution)/shard_map/pallas_call | solution.py:273
Async XLA Ops:
  35.2 11.1 %collective-permute-start = (bf16[128,1024]{1,0:T(8,128)(2,1)S(1)}, bf16[128,1024]{1,0:T(8,128)(2,1)S(1)}, u32[]{:S(2)}, u32[]{:S(2)}) collective-permute-start(bf16[128,1024]{1,0:T(8,128)(2,1)S(1)} %slice.4), channel_id=1, source_target_pairs={{0,16},{16,0},{1,17},{17,1},{2,18},{18,2},{3,19},{19,3},{4,20},{20... | collective-permute-start | bytes 786440 | tf_op jit(solution)/shard_map/ppermute | solution.py:269
  46.3 0.7 %copy-start = (bf16[128,1024]{1,0:T(8,128)(2,1)}, bf16[128,1024]{1,0:T(8,128)(2,1)S(1)}, u32[]{:S(2)}) copy-start(bf16[128,1024]{1,0:T(8,128)(2,1)S(1)} %collective-permute-done.other_ref) | copy-start | bytes 786436
